TPU v7x, 128 devices: a whole 4x4x4 slice. The times are simulated.
128 devices in a mesh: pts: 32 (over y, z, core), grp: 4 (over x).
Axes of the slice: x: 4, y: 4, z: 4, core: 2. Of those that a mesh axis runs over, the one named last changes fastest.
Arguments:
- coords: float32 [3, 65536], P(None, ('pts', 'grp')), may hold values from 0 to 1, as said below
- observations: float32 [65536], P(('pts', 'grp')), may hold values from -18 to 18
- length_scales: float32 [3], replicated, may hold values from 0.3 to 1
- nugget: float32 [1], replicated, may hold values from 0.05 to 0.3
- fetch_table: int32 [128, 128, 11], P(('pts', 'grp')), may hold values from 0 to 511
- slot_of: int32 [30, 65536], P(None, ('pts', 'grp')), may hold values from 0 to 2943, as said below
Outputs:
- whitened: float32 [65536], P(('pts', 'grp'))
- neg_loglik: float32 [], replicated
Inputs may be any that keep to these rules, and one draw needn't show every extreme that they name: `coords`: the points of the device of tile t and slab s have first coordinate in [t / 32, (t + 1) / 32) and time coordinate in [s / 4, (s + 1) / 4). `slot_of`: the 30 slots of one point are distinct. Slots below 1536 never point before the first tile or after the last one. Only the first 32 points of each device use slots of 1536 or more, and each of those slots is used at most once on its device; on every device some owner's 11 far slots are all used.
All inputs are finite; a program needn't handle non-finite values.
Results may differ from a plain program's by a relative error of at most 0.0003.
Values sent between devices are 32-bit elements; how exact they have to be, the bound alone decides.
A program may use at most 128 MiB of HBM per device.

v0:
```python
import jax
import jax.numpy as jnp
from jax import lax
from jax.sharding import Mesh
from jax.sharding import PartitionSpec as P

PTS = ("pts_0", "pts_1", "pts_2")
PTS_GRP = ("pts_0", "pts_1", "pts_2", "grp")


root_three = 1.7320508075688772
half_log_tau = 0.9189385332046727


def extended(cells, sides, width):
    for axis, dim in sides:
        count = lax.axis_size(axis)
        ends = count - 1
        head = lax.slice_in_dim(cells, 0, width, axis=dim)
        tail = lax.slice_in_dim(cells, cells.shape[dim] - width, cells.shape[dim], axis=dim)
        cells = jnp.concatenate(
            [
                lax.ppermute(tail, axis, [(i, (i + 1) % count) for i in range(ends)]),
                cells,
                lax.ppermute(head, axis, [((i + 1) % count, i) for i in range(ends)]),
            ],
            axis=dim,
        )
    return cells


def by_axis(array, axes):
    for axis in axes:
        array = lax.psum(array, axis)
    return array


def covariance(points, inverse_lengths, nugget):
    scaled = points * inverse_lengths[:, None, None]
    gap = scaled[:, :, None, :] - scaled[:, None, :, :]
    distance = jnp.sqrt(jnp.sum(gap * gap, axis=0))
    scaled_distance = root_three * distance
    order = points.shape[1]
    identity = jnp.eye(order, dtype=jnp.float32)[:, :, None]
    return (1.0 + scaled_distance) * jnp.exp(-scaled_distance) + nugget[0] * identity


def eliminate(matrix, values):
    order = matrix.shape[0]
    for step in range(order):
        pivot = jnp.sqrt(matrix[0, 0])
        solved = values[0] / pivot
        if step == order - 1:
            return (solved, pivot)
        column = matrix[1:, 0] / pivot
        matrix = matrix[1:, 1:] - column[:, None, :] * column[None, :, :]
        values = values[1:] - column * solved


def split_three(table):
    upper = table.astype(jnp.bfloat16)
    rest = table - lax.optimization_barrier(upper).astype(jnp.float32)
    middle = rest.astype(jnp.bfloat16)
    lower = (rest - lax.optimization_barrier(middle).astype(jnp.float32)).astype(jnp.bfloat16)
    return jnp.concatenate([upper, middle, lower], axis=0)


def select_slots(table, slot_of):
    pieces = split_three(table)
    width = table.shape[0]
    rows = jnp.arange(table.shape[1], dtype=jnp.int32)[:, None]

    def one_neighbour(indices):
        picker = (rows == indices[None, :]).astype(jnp.bfloat16)
        product = jnp.dot(pieces, picker, preferred_element_type=jnp.float32)
        return product[:width] + (product[width : 2 * width] + product[2 * width :])

    picked = lax.map(one_neighbour, slot_of)
    return jnp.transpose(picked, (1, 0, 2))


def body(coords, observations, length_scales, nugget, fetch_table, slot_of):
    local_count = coords.shape[1]
    owners = fetch_table.shape[1]
    capacity = fetch_table.shape[2]
    my_table = fetch_table[0]
    payload = jnp.concatenate([coords, observations[None, :]], axis=0)
    near = extended(payload, ((PTS, 1),), local_count)
    wanted = lax.all_to_all(my_table, PTS_GRP, split_axis=0, concat_axis=0, tiled=True)
    served = jnp.take(payload, wanted, axis=1)
    buffer = lax.all_to_all(served, PTS_GRP, split_axis=1, concat_axis=1, tiled=True)
    slots = jnp.concatenate([near, buffer.reshape(4, owners * capacity)], axis=1)
    gathered = select_slots(slots, slot_of)
    members = jnp.concatenate([gathered, payload[:, None, :]], axis=1)
    matrix = covariance(members[:3], 1.0 / length_scales, nugget)
    whitened, pivot = eliminate(matrix, members[3])
    partial_value = jnp.sum(2.0 * jnp.log(pivot) + whitened * whitened)
    total = by_axis(partial_value, PTS_GRP)
    everyone = local_count * lax.axis_size(PTS) * lax.axis_size("grp")
    neg_loglik = total / (2.0 * everyone) + half_log_tau
    return (whitened, neg_loglik)


def solution(mesh):
    split = Mesh(
        mesh.devices.reshape(4, 4, 2, mesh.shape["grp"]), ("pts_0", "pts_1", "pts_2", "grp")
    )
    placed = (P(None, PTS_GRP), P(PTS_GRP), P(), P(), P(PTS_GRP, None, None), P(None, PTS_GRP))
    return jax.shard_map(
        body, mesh=split, in_specs=placed, out_specs=(P(PTS_GRP), P()), check_vma=False
    )
```

profile of v0, /device:TPU:0, one launch (start us, length us, event | category | flops | bytes accessed | tf_op | source)
XLA Modules:
  0.0 151.5 jit_solution(11847054878074390985)
XLA Ops:
  1.4 1.3 collective-permute-start.1
  2.6 3.0 %collective-permute-start = (f32[4,512]{1,0:T(4,128)S(1)}, f32[4,512]{1,0:T(4,128)S(1)}, u32[]{:S(2)}, u32[]{:S(2)}) collective-permute-start(f32[4,512]{1,0:T(4,128)S(1)} %pad_maximum_fusion.3), channel_id=1, source_target_pairs={{0,4},{4,8},{8,12},{12,16},{16,20},{20,24},{24,28},{28,32},{32,36}... | collective-permute-start | bytes 24584 | tf_op jit(solution)/shard_map/ppermute | solution.py:23
  5.7 1.4 copy.55
  7.1 14.0 %all-to-all-start = ((s32[128,1,11]{2,1,0:T(1,128)}), s32[128,1,11]{2,1,0:T(1,128)S(1)}, u32[]{:S(2)}, u32[]{:S(2)}) async-start(s32[128,1,11]{2,1,0:T(1,128)} %copy.55), calls=%async_computation | async-start | bytes 131072 | tf_op jit(solution)/shard_map/all_to_all | solution.py:89
  22.5 7.8 %all-to-all-done = s32[128,1,11]{2,1,0:T(1,128)S(1)} async-done(((s32[128,1,11]{2,1,0:T(1,128)}), s32[128,1,11]{2,1,0:T(1,128)S(1)}, u32[]{:S(2)}, u32[]{:S(2)}) %all-to-all-start) | async-done | bytes 5664 | tf_op jit(solution)/shard_map/all_to_all | solution.py:89
  30.9 2.7 %gather_fusion = f32[1408,4]{1,0:T(8,128)S(1)} fusion(f32[4,512]{0,1:T(8,128)S(1)} %copy.60, s32[2048]{0:T(1024)S(1)} %pad_clamp_fusion), kind=kCustom, calls=%fused_computation | custom fusion | bytes 50688 | tf_op jit(solution)/shard_map/jit(_take)/gather | solution.py:90
  34.2 0.9 copy.62
  35.1 4.9 %all-to-all-start.1 = ((f32[4,128,11]{2,0,1:T(4,128)}), f32[4,128,11]{2,0,1:T(4,128)S(1)}, u32[]{:S(2)}, u32[]{:S(2)}) async-start(f32[4,128,11]{2,0,1:T(4,128)} %copy.62), calls=%async_computation.1 | async-start | bytes 524288 | tf_op jit(solution)/shard_map/all_to_all | solution.py:91
  40.0 10.3 %all-to-all-done.1 = f32[4,128,11]{2,0,1:T(4,128)S(1)} async-done(((f32[4,128,11]{2,0,1:T(4,128)}), f32[4,128,11]{2,0,1:T(4,128)S(1)}, u32[]{:S(2)}, u32[]{:S(2)}) %all-to-all-start.1) | async-done | bytes 22560 | tf_op jit(solution)/shard_map/all_to_all | solution.py:91
  50.7 57.3 %while.11 = (s32[]{:T(128)}, f32[30,4,512]{2,0,1:T(8,128)S(1)}, s32[30,512]{1,0:T(8,128)}, bf16[12,2944]{1,0:T(8,128)(2,1)S(1)}, s32[]{:T(128)}, /*index=5*/s32[]{:T(128)}) while((s32[]{:T(128)}, f32[30,4,512]{2,0,1:T(8,128)S(1)}, s32[30,512]{1,0:T(8,128)}, bf16[12,2944]{1,0:T(8,128)(2,1)S(1)}, s32[]{:T(128)}, ...), condition=%wide.region_1.2_spmd.clone, body=%wide.region_0.1_spmd.clone.sunk | while | flops 37687296 | bytes 166997 | solution.py:78
  50.7 0.7 constant_dynamic-slice_fusion.2
  51.5 1.1 fusion.58
  52.6 0.7 constant_dynamic-slice_fusion.2
  53.4 1.1 fusion.58
  54.6 0.7 constant_dynamic-slice_fusion.2
  55.3 1.1 fusion.58
  56.5 0.7 constant_dynamic-slice_fusion.2
  57.2 1.1 fusion.58
  58.4 0.7 constant_dynamic-slice_fusion.2
  59.1 1.1 fusion.58
  60.3 0.7 constant_dynamic-slice_fusion.2
  61.0 1.1 fusion.58
  62.2 0.7 constant_dynamic-slice_fusion.2
  62.9 1.1 fusion.58
  64.1 0.7 constant_dynamic-slice_fusion.2
  64.8 1.1 fusion.58
  66.0 0.7 constant_dynamic-slice_fusion.2
  66.8 1.1 fusion.58
  67.9 0.7 constant_dynamic-slice_fusion.2
  68.7 1.1 fusion.58
  69.8 0.7 constant_dynamic-slice_fusion.2
  70.6 1.1 fusion.58
  71.8 0.7 constant_dynamic-slice_fusion.2
  72.5 1.1 fusion.58
  73.7 0.7 constant_dynamic-slice_fusion.2
  74.4 1.1 fusion.58
  75.6 0.7 constant_dynamic-slice_fusion.2
  76.3 1.1 fusion.58
  77.5 0.7 constant_dynamic-slice_fusion.2
  78.2 1.1 fusion.58
  80.1 1.1 fusion.58
  81.3 0.7 constant_dynamic-slice_fusion.2
  82.0 1.1 fusion.58
  83.2 0.7 constant_dynamic-slice_fusion.2
  84.0 1.1 fusion.58
  85.9 1.1 fusion.58
  87.8 1.1 fusion.58
  89.7 1.1 fusion.58
  91.6 1.1 fusion.58
  93.5 1.1 fusion.58
  95.4 1.1 fusion.58
  97.3 1.1 fusion.58
  99.2 1.1 fusion.58
  101.2 1.1 fusion.58
  103.1 1.1 fusion.58
  105.0 1.1 fusion.58
  106.9 1.1 fusion.58
  108.2 0.7 multiply_reduce_fusion
  108.9 0.9 multiply_add_fusion
  117.3 1.2 add_reduce_fusion
  118.5 9.4 %psum.28 = f32[]{:T(128)} all-reduce(f32[]{:T(128)} %get-tuple-element.48), channel_id=1, replica_groups=mesh['pts_0'=4,'pts_1'=4,'pts_2'=2,'grp'=4] {'pts_0'}, use_global_device_ids=true, to_apply=%region_4.5 | all-reduce | flops 1 | bytes 8 | tf_op jit(solution)/shard_map/psum | solution.py:34
  127.9 9.5 %psum.29 = f32[]{:T(128)} all-reduce(f32[]{:T(128)} %psum.28), channel_id=1, replica_groups=mesh['pts_0'=4,'pts_1'=4,'pts_2'=2,'grp'=4] {'pts_1'}, use_global_device_ids=true, to_apply=%region_5.6 | all-reduce | flops 1 | bytes 8 | tf_op jit(solution)/shard_map/psum | solution.py:34
  137.4 3.1 %psum.30 = f32[]{:T(128)} all-reduce(f32[]{:T(128)} %psum.29), channel_id=1, replica_groups=mesh['pts_0'=4,'pts_1'=4,'pts_2'=2,'grp'=4] {'pts_2'}, use_global_device_ids=true, to_apply=%region_6.7 | all-reduce | flops 1 | bytes 8 | tf_op jit(solution)/shard_map/psum | solution.py:34
  140.5 9.2 %psum.31 = f32[]{:T(128)} all-reduce(f32[]{:T(128)} %psum.30), channel_id=1, replica_groups=mesh['pts_0'=4,'pts_1'=4,'pts_2'=2,'grp'=4] {'grp'}, use_global_device_ids=true, to_apply=%region_7.8 | all-reduce | flops 1 | bytes 8 | tf_op jit(solution)/shard_map/psum | solution.py:34
  (309 shorter events, 21.8 us)
Async XLA Ops:
  1.4 49.2 %collective-permute-start.1 = (f32[4,512]{1,0:T(4,128)S(1)}, f32[4,512]{1,0:T(4,128)S(1)}, u32[]{:S(2)}, u32[]{:S(2)}) collective-permute-start(f32[4,512]{1,0:T(4,128)S(1)} %pad_maximum_fusion.3), channel_id=1, source_target_pairs={{4,0},{8,4},{12,8},{16,12},{20,16},{24,20},{28,24},{32,28},{36,32}... | collective-permute-start | bytes 24584 | tf_op jit(solution)/shard_map/ppermute | solution.py:25
  2.6 47.9 %collective-permute-start = (f32[4,512]{1,0:T(4,128)S(1)}, f32[4,512]{1,0:T(4,128)S(1)}, u32[]{:S(2)}, u32[]{:S(2)}) collective-permute-start(f32[4,512]{1,0:T(4,128)S(1)} %pad_maximum_fusion.3), channel_id=1, source_target_pairs={{0,4},{4,8},{8,12},{12,16},{16,20},{20,24},{24,28},{28,32},{32,36}... | collective-permute-start | bytes 24584 | tf_op jit(solution)/shard_map/ppermute | solution.py:23
  7.1 23.2 %all-to-all-start = ((s32[128,1,11]{2,1,0:T(1,128)}), s32[128,1,11]{2,1,0:T(1,128)S(1)}, u32[]{:S(2)}, u32[]{:S(2)}) async-start(s32[128,1,11]{2,1,0:T(1,128)} %copy.55), calls=%async_computation | async-start | bytes 131072 | tf_op jit(solution)/shard_map/all_to_all | solution.py:89
  33.6 16.9 %copy-start = (f32[3,512]{1,0:T(4,128)S(1)}, f32[3,512]{1,0:T(4,128)}, u32[]{:S(2)}) copy-start(f32[3,512]{1,0:T(4,128)} %param.8) | copy-start | bytes 18436
  33.7 16.9 %copy-start.1 = (f32[512]{0:T(512)S(1)}, f32[512]{0:T(512)}, u32[]{:S(2)}) copy-start(f32[512]{0:T(512)} %param.9) | copy-start | bytes 6148
  35.1 15.2 %all-to-all-start.1 = ((f32[4,128,11]{2,0,1:T(4,128)}), f32[4,128,11]{2,0,1:T(4,128)S(1)}, u32[]{:S(2)}, u32[]{:S(2)}) async-start(f32[4,128,11]{2,0,1:T(4,128)} %copy.62), calls=%async_computation.1 | async-start | bytes 524288 | tf_op jit(solution)/shard_map/all_to_all | solution.py:91
where the time goes:
time: 154 us; the launch traced here: 151 us
  local copies, waits for them, and re-layouts  31.9 us (21%)
  matrix products  31.5 us (20%)
  blocking collectives  31.2 us (20%)
  starting transfers between devices  23.2 us (15%)
  waiting for transfers between devices  18 us (12%)
  other arithmetic  10.1 us (7%)
  between operations  4.65 us (3%)
    dot_general x30, matrix products, one_neighbour(): product = jnp.dot(pieces, picker, preferred_element_type=jnp.float32)  31.5 us
    psum x4, blocking collectives, by_axis(): array = lax.psum(array, axis)  31.2 us
    dynamic_slice x30, local copies, waits for them, and re-layouts, select_slots(): picked = lax.map(one_neighbour, slot_of)  21.8 us
    all_to_all x1, starting transfers between devices, body(): lax.all_to_all(my_table, PTS_GRP, split_axis=0, concat_axis=0, tiled=True)  14 us
    all_to_all x1, waiting for transfers between devices, body(): lax.all_to_all(served, PTS_GRP, split_axis=1, concat_axis=1, tiled=True)  10.3 us
    all_to_all x1, waiting for transfers between devices, body(): lax.all_to_all(my_table, PTS_GRP, split_axis=0, concat_axis=0, tiled=True)  7.75 us
    all_to_all x1, starting transfers between devices, body(): lax.all_to_all(served, PTS_GRP, split_axis=1, concat_axis=1, tiled=True)  4.91 us
    sub x29, other arithmetic, eliminate(): matrix = matrix[1:, 1:] - column[:, None, :] * column[None, :, :]  4.27 us
  transfers between devices with their start and end apart: 4, of which 2 were waited for; matrix products, arithmetic and copies ran while one was open for 5% of the time, Pallas kernels for 0%

commit v1 on v0

v1 whole, which is shorter than its diff:
```python
import functools

import jax
import jax.numpy as jnp
from jax import lax
from jax.experimental import pallas as pl
from jax.experimental.pallas import tpu as pltpu
from jax.sharding import PartitionSpec as P

ALL = ("pts", "grp")
MESH = pl.DeviceIdType.MESH

root_three = 1.7320508075688772
half_log_tau = 0.9189385332046727

POINTS = 512
LANES = 128
CHUNKS = POINTS // LANES
ORDER = 31
CAP = 11
NEAR = 3 * POINTS
DEVICES = 128


def hops(offset):
    y, z, core, x = offset
    ring = (0, 1, 2, 1)
    return ring[y] + ring[z] + ring[x] + 0.3 * core


def far_first(offsets):
    return sorted(offsets, key=lambda offset: -hops(offset))


EVERYONE = far_first(
    (y, z, core, x)
    for y in range(4)
    for z in range(4)
    for core in range(2)
    for x in range(4)
    if (y, z, core, x) != (0, 0, 0, 0)
)
PLANE = [offset for offset in EVERYONE if offset[2:] == (0, 0)]
GROUP = [offset for offset in EVERYONE if offset[:2] == (0, 0)]


def spread(row, shape):
    return jnp.broadcast_to(row, shape)


def lanes_of(row, lane):
    return jnp.take_along_axis(
        spread(row, lane.shape), lane, axis=1, mode="promise_in_bounds"
    )


def eliminate(scaled, observed, nugget, held, eliminated, chunk_ref):
    coords, _ = held
    tile = (8, LANES)
    sub = lax.broadcasted_iota(jnp.int32, tile, 0)
    for panel in range(4):
        first = 8 * panel
        members = range(first, min(first + 8, ORDER))
        tiles = range(panel, 4)
        rows = {}
        for a in members:
            here = [spread(coords[c, a : a + 1, :], tile) for c in range(4)]
            for t in tiles:
                square = None
                for c in range(3):
                    gap = scaled[c][8 * t : 8 * t + 8] - here[c]
                    square = gap * gap if square is None else square + gap * gap
                square = jnp.maximum(square, 1e-36)
                distance = square * lax.rsqrt(square)
                value = (1.0 + distance) * jnp.exp(-distance)
                if t == panel:
                    value = jnp.where(sub == a - first, value + nugget, value)
                if t == 3:
                    value = jnp.where(sub == 7, here[3], value)
                rows[a, t] = value
        for k in range(first):
            column = {t: eliminated[k, t] for t in tiles}
            for a in members:
                factor = spread(eliminated[k, panel, a - first : a - first + 1, :], tile)
                for t in tiles:
                    rows[a, t] = rows[a, t] - factor * column[t]
        for k in members:
            pivot = rows[k, panel][k - first : k - first + 1, :]
            if k == ORDER - 1:
                solved = rows[k, 3][7:8, :] * lax.rsqrt(pivot)
                chunk_ref[...] = solved
                return jnp.log(pivot) + solved * solved
            inverse = lax.rsqrt(spread(pivot, tile))
            column = {t: rows[k, t] * inverse for t in tiles}
            for t in tiles:
                if t > panel:
                    eliminated[k, t] = column[t]
            for a in range(k + 1, members[-1] + 1):
                factor = spread(column[panel][a - first : a - first + 1, :], tile)
                for t in tiles:
                    rows[a, t] = rows[a, t] - factor * column[t]


def kernel(
    coords_hbm, obs_hbm, scales_hbm, nugget_hbm, fetch_hbm, slot_hbm,
    white_hbm, nll_hbm,
    coords, obs, fetch, slots, scales, nugget_s, held, eliminated, white, reply, far, part, reduced, nll,
    local_sem, group_send, group_recv, request_sem, reply_sem, reduce_sem, out_sem,
):
    pts, x = lax.axis_index("pts"), lax.axis_index("grp")
    s, core = pts // 2, pts % 2
    y, z = s // 4, s % 4
    me = 8 * s + 4 * core + x
    mine = 4 * core + x

    def device(offset):
        dy, dz, dcore, dx = offset
        return ((((y + dy) % 4) * 4 + (z + dz) % 4) * 2 + (core + dcore) % 2, (x + dx) % 4)

    across = ((((s + 2 * core + 15) % 16) * 2 + 1 - core), x)

    barrier = pltpu.get_barrier_semaphore()
    peers = [device(o) for o in PLANE] + [device(o) for o in GROUP] + [across]
    for peer in peers:
        pl.semaphore_signal(barrier, 1, device_id=peer, device_id_type=MESH)

    loads = [
        pltpu.make_async_copy(fetch_hbm, fetch.at[s], local_sem.at[0]),
        pltpu.make_async_copy(coords_hbm, coords.at[mine], local_sem.at[1]),
        pltpu.make_async_copy(obs_hbm, obs.at[mine], local_sem.at[2]),
        pltpu.make_async_copy(slot_hbm, slots, local_sem.at[3]),
        pltpu.make_async_copy(scales_hbm, scales, local_sem.at[4]),
        pltpu.make_async_copy(nugget_hbm, nugget_s, local_sem.at[5]),
    ]
    for load in loads:
        load.start()
    for load in loads:
        load.wait()
    pl.semaphore_wait(barrier, len(peers))

    def remote(src, dst, send, recv, peer):
        return pltpu.make_async_remote_copy(
            src_ref=src, dst_ref=dst, send_sem=send, recv_sem=recv, device_id=peer, device_id_type=MESH
        )

    for offset in PLANE:
        remote(fetch.at[s], fetch.at[s], request_sem.at[0], request_sem.at[1], device(offset)).start()
    for peer, slot in [(across, 8)] + [(device(o), mine) for o in GROUP]:
        remote(coords.at[mine], coords.at[slot], group_send.at[0], group_recv.at[slot, 0], peer).start()
        remote(obs.at[mine], obs.at[slot], group_send.at[1], group_recv.at[slot, 1], peer).start()

    def arrived(slot):
        pltpu.make_async_copy(coords.at[slot], coords.at[slot], group_recv.at[slot, 0]).wait()
        pltpu.make_async_copy(obs.at[slot], obs.at[slot], group_recv.at[slot, 1]).wait()

    def table_row(slot, c, block):
        if c == 3:
            return obs[slot, block : block + 1, :]
        return coords[slot, c : c + 1, block * LANES : (block + 1) * LANES]

    tile = (8, LANES)
    factor = [jnp.float32(root_three) / jnp.full((1, LANES), scales[c], jnp.float32) for c in range(3)]
    nugget = nugget_s[0]
    before = core * x + (1 - core) * 8
    after = core * 8 + (1 - core) * (4 + x)

    def near_rows(index):
        block, lane = index >> 7, index & 127
        found = [jnp.zeros(index.shape, jnp.float32) for _ in range(4)]
        for r in range(12):
            at = block == r
            slot = (before, mine, after)[r // 4]
            for c in range(4):
                found[c] = jnp.where(at, lanes_of(table_row(slot, c, r % 4), lane), found[c])
        return found

    def finish(found, chunk):
        scaled = [found[c] * factor[c] for c in range(3)]
        for c in range(3):
            held[c] = scaled[c]
        held[3] = found[3]
        return eliminate(scaled, found[3], nugget, (held, None), eliminated, white.at[pl.ds(chunk, 1), :])

    def index_of(chunk):
        itself = POINTS + chunk * LANES + lax.broadcasted_iota(jnp.int32, (2, LANES), 1)
        listed = slots[:, pl.ds(pl.multiple_of(chunk * LANES, LANES), LANES)]
        return jnp.concatenate([listed, itself], axis=0)

    def near_chunk(chunk, total):
        return total + finish(near_rows(index_of(chunk)), chunk)

    arrived((1 - core) * 4 + x)
    arrived(8)
    total = near_chunk(1, jnp.zeros((1, LANES), jnp.float32))

    for offset in GROUP:
        _, _, dcore, dx = offset
        if (dcore, dx) != (1, 0):
            arrived(((core + dcore) % 2) * 4 + (x + dx) % 4)
    pltpu.make_async_copy(fetch.at[pl.ds(0, 15)], fetch.at[pl.ds(0, 15)], request_sem.at[1]).wait()
    lane_id = lax.broadcasted_iota(jnp.int32, (16, LANES), 1)
    wanted = jnp.zeros((16, LANES), jnp.int32)
    for q in range(16):
        asked = jnp.concatenate([fetch[q], jnp.zeros((5, LANES), jnp.int32)], axis=0)
        asked = pltpu.roll(asked, (8 * q - 8 * s + LANES) % LANES, axis=1)
        wanted = jnp.where(lane_id // 8 == q, asked, wanted)
    owner_block, lane = (lane_id % 8) * 4 + (wanted >> 7), wanted & 127
    served = [jnp.zeros((16, LANES), jnp.float32) for _ in range(4)]
    for r in range(32):
        at = owner_block == r
        for c in range(4):
            served[c] = jnp.where(at, lanes_of(table_row(r // 4, c, r % 4), lane), served[c])
    stacked = jnp.concatenate(served + [jnp.zeros((64, LANES), jnp.float32)], axis=0)
    reply[...] = stacked.T
    far[pl.ds(pl.multiple_of(8 * s, 8), 8), :] = reply[pl.ds(pl.multiple_of(8 * s, 8), 8), :]
    for offset in PLANE:
        peer = device(offset)
        there = peer[0] // 2
        remote(
            reply.at[pl.ds(pl.multiple_of(8 * there, 8), 8), :],
            far.at[pl.ds(pl.multiple_of(8 * s, 8), 8), :],
            reply_sem.at[0], reply_sem.at[1], peer,
        ).start()

    total = lax.fori_loop(2, CHUNKS, near_chunk, total)
    index = index_of(0)
    found = near_rows(index)

    pltpu.make_async_copy(far.at[pl.ds(0, 120)], far.at[pl.ds(0, 120)], reply_sem.at[1]).wait()
    table = far[...].T
    number = index - NEAR
    owner = (number * 5958) >> 16
    place = jnp.where(number >= 0, number - CAP * owner, -1)
    owner = owner & 127
    for r in range(CAP):
        at = place == r
        for c in range(4):
            row = table[16 * c + r : 16 * c + r + 1, :]
            found[c] = jnp.where(at, lanes_of(row, owner), found[c])
    total = total + finish(found, 0)

    out = pltpu.make_async_copy(white, white_hbm, out_sem.at[0])
    out.start()
    part[0] = total
    reduced[me] = total
    for offset in EVERYONE:
        remote(part.at[0], reduced.at[me], reduce_sem.at[0], reduce_sem.at[1], device(offset)).start()
    pltpu.make_async_copy(reduced.at[pl.ds(0, 127)], reduced.at[pl.ds(0, 127)], reduce_sem.at[1]).wait()
    everything = jnp.sum(reduced[...], axis=0)
    scale = 1.0 / (2.0 * POINTS * DEVICES)
    nll[...] = jnp.full((1, LANES), jnp.sum(everything) * scale + half_log_tau, jnp.float32)
    nll_out = pltpu.make_async_copy(nll, nll_hbm, out_sem.at[1])
    nll_out.start()

    pltpu.make_async_copy(fetch.at[pl.ds(0, 15)], fetch.at[pl.ds(0, 15)], request_sem.at[0]).wait()
    pltpu.make_async_copy(coords.at[pl.ds(0, 8)], coords.at[pl.ds(0, 8)], group_send.at[0]).wait()
    pltpu.make_async_copy(obs.at[pl.ds(0, 8)], obs.at[pl.ds(0, 8)], group_send.at[1]).wait()
    pltpu.make_async_copy(far.at[pl.ds(0, 120)], far.at[pl.ds(0, 120)], reply_sem.at[0]).wait()
    pltpu.make_async_copy(reduced.at[pl.ds(0, 127)], reduced.at[pl.ds(0, 127)], reduce_sem.at[0]).wait()
    out.wait()
    nll_out.wait()


def body(coords, observations, length_scales, nugget, fetch_table, slot_of):
    anywhere = pl.BlockSpec(memory_space=pl.ANY)
    white, nll = pl.pallas_call(
        kernel,
        out_shape=(
            jax.ShapeDtypeStruct((CHUNKS, LANES), jnp.float32),
            jax.ShapeDtypeStruct((1, LANES), jnp.float32),
        ),
        in_specs=[anywhere] * 6,
        out_specs=(anywhere, anywhere),
        scratch_shapes=[
            pltpu.VMEM((9, 3, POINTS), jnp.float32),
            pltpu.VMEM((9, CHUNKS, LANES), jnp.float32),
            pltpu.VMEM((16, CAP, LANES), jnp.int32),
            pltpu.VMEM((ORDER - 1, POINTS), jnp.int32),
            pltpu.SMEM((3,), jnp.float32),
            pltpu.SMEM((1,), jnp.float32),
            pltpu.VMEM((4, 32, LANES), jnp.float32),
            pltpu.VMEM((ORDER, 4, 8, LANES), jnp.float32),
            pltpu.VMEM((CHUNKS, LANES), jnp.float32),
            pltpu.VMEM((128, LANES), jnp.float32),
            pltpu.VMEM((128, LANES), jnp.float32),
            pltpu.VMEM((1, 1, LANES), jnp.float32),
            pltpu.VMEM((DEVICES, 1, LANES), jnp.float32),
            pltpu.VMEM((1, LANES), jnp.float32),
            pltpu.SemaphoreType.DMA((6,)),
            pltpu.SemaphoreType.DMA((2,)),
            pltpu.SemaphoreType.DMA((9, 2)),
            pltpu.SemaphoreType.DMA((2,)),
            pltpu.SemaphoreType.DMA((2,)),
            pltpu.SemaphoreType.DMA((2,)),
            pltpu.SemaphoreType.DMA((2,)),
        ],
        compiler_params=pltpu.CompilerParams(collective_id=0, has_side_effects=True),
        name="vecchia",
    )(
        coords,
        observations.reshape(CHUNKS, LANES),
        length_scales,
        nugget,
        jnp.transpose(fetch_table, (2, 0, 1)).reshape(CAP, LANES),
        slot_of,
    )
    return white.reshape(POINTS), nll[0, 0]


def solution(mesh):
    return jax.shard_map(
        body,
        mesh=mesh,
        in_specs=(P(None, ALL), P(ALL), P(), P(), P(ALL, None, None), P(None, ALL)),
        out_specs=(P(ALL), P()),
        check_vma=False,
    )
```

time: 154 us -> 31 us (0.20)
  the two profiles are of different devices: /device:TPU:0 before, /device:TPU:1 now
where the time goes in v1:
time: 31 us; the launch traced here: 30.8 us
  Pallas kernels  25.8 us (83%)
  local copies, waits for them, and re-layouts  2.54 us (8%)
  between operations  2.46 us (8%)
    pallas_call x1, Pallas kernels, body(): pl.pallas_call(kernel, out_shape=(jax.ShapeDtypeStruct((CHUNKS, LANES), j...  25.8 us
    unnamed x6, local copies, waits for them, and re-layouts  2.54 us

profile of v1, /device:TPU:1, one launch (start us, length us, event | category | flops | bytes accessed | tf_op | source)
XLA Modules:
  0.0 30.8 jit_solution(18314236988487517864)
XLA Ops:
  1.3 1.3 %copy.10 = s32[1,128,11]{1,2,0:T(8,128)} copy(s32[1,128,11]{1,0,2:T(1,128)} %param.10) | data formatting | bytes 11264 | tf_op args[4]
  2.6 25.8 %vecchia.1 = (f32[4,128]{1,0:T(4,128)}, f32[1,128]{1,0:T(1,128)}) custom-call(f32[3,512]{1,0:T(4,128)} %coords_hbm.1, f32[4,128]{1,0:T(4,128)} %bitcast.10, f32[3]{0:T(128)} %scales_hbm.1, f32[1]{0:T(128)S(6)} %copy.13.nugget_hbm, s32[11,128]{1,0:T(8,128)} %bitcast.9, s32[30,512]{1,0:T(8,128)} %slot_hbm.1), custom_call_target="tpu_custom_call" | custom-call | tf_op jit(solution)/shard_map/vecchia/pallas_call | solution.py:266
  28.3 0.0 copy-start
  28.4 0.6 %copy-done = f32[4,128]{1,0:T(4,128)S(1)} copy-done((f32[4,128]{1,0:T(4,128)S(1)}, f32[4,128]{1,0:T(4,128)}, u32[]{:S(2)}) %copy-start) | copy-done | bytes 2072
  29.0 0.0 copy-start.1
  29.0 0.6 %copy.14 = f32[512]{0:T(512)} copy(f32[512]{0:T(512)S(1)} %bitcast.11) | data formatting | bytes 4096
  29.6 0.0 copy-done.1
Async XLA Ops:
  28.3 0.7 %copy-start = (f32[4,128]{1,0:T(4,128)S(1)}, f32[4,128]{1,0:T(4,128)}, u32[]{:S(2)}) copy-start(f32[4,128]{1,0:T(4,128)} %get-tuple-element.4) | copy-start | bytes 6148
  29.0 0.6 %copy-start.1 = (f32[1,128]{1,0:T(1,128)S(1)}, f32[1,128]{1,0:T(1,128)}, u32[]{:S(2)}) copy-start(f32[1,128]{1,0:T(1,128)} %get-tuple-element.5) | copy-start | bytes 1540

commit v2 on v1

v2 whole, which is shorter than its diff:
```python
import jax
import jax.numpy as jnp
from jax import lax
from jax.experimental import pallas as pl
from jax.experimental.pallas import tpu as pltpu
from jax.sharding import PartitionSpec as P

ALL = ("pts", "grp")
MESH = pl.DeviceIdType.MESH

root_three = 1.7320508075688772
half_log_tau = 0.9189385332046727

POINTS = 512
LANES = 128
CHUNKS = POINTS // LANES
ORDER = 31
CAP = 11
EARLY = 32
NEAR = 3 * POINTS
DEVICES = 128
TILE = (8, LANES)


def hops(offset):
    y, z, core, x = offset
    ring = (0, 1, 2, 1)
    return ring[y] + ring[z] + ring[x] + 0.3 * core


EVERYONE = sorted(
    (
        (y, z, core, x)
        for y in range(4)
        for z in range(4)
        for core in range(2)
        for x in range(4)
        if (y, z, core, x) != (0, 0, 0, 0)
    ),
    key=lambda offset: -hops(offset),
)
PLANE = [offset for offset in EVERYONE if offset[2:] == (0, 0)]
GROUP = [offset for offset in EVERYONE if offset[:2] == (0, 0)]


def spread(row, shape):
    return jnp.broadcast_to(row, shape)


def lanes_of(rows, lane):
    return jnp.take_along_axis(spread(rows, lane.shape), lane, axis=1, mode="promise_in_bounds")


def eliminate(scaled, nugget, held, eliminated, white_ref):
    sub = lax.broadcasted_iota(jnp.int32, TILE, 0)
    for panel in range(4):
        first = 8 * panel
        members = range(first, min(first + 8, ORDER))
        tiles = range(panel, 4)
        rows = {}
        for a in members:
            here = [spread(held[c, a : a + 1, :], TILE) for c in range(4)]
            for t in tiles:
                square = None
                for c in range(3):
                    gap = scaled[c][8 * t : 8 * t + 8] - here[c]
                    square = gap * gap if square is None else square + gap * gap
                square = jnp.maximum(square, 1e-36)
                distance = square * lax.rsqrt(square)
                value = (1.0 + distance) * jnp.exp(-distance)
                if t == panel:
                    value = jnp.where(sub == a - first, value + nugget, value)
                if t == 3:
                    value = jnp.where(sub == 7, here[3], value)
                rows[a, t] = value
        for k in range(first):
            column = {t: eliminated[k, t] for t in tiles}
            for a in members:
                factor = spread(eliminated[k, panel, a - first : a - first + 1, :], TILE)
                for t in tiles:
                    rows[a, t] = rows[a, t] - factor * column[t]
        for k in members:
            pivot = rows[k, panel][k - first : k - first + 1, :]
            if k == ORDER - 1:
                solved = rows[k, 3][7:8, :] * lax.rsqrt(pivot)
                white_ref[...] = solved
                return jnp.log(pivot) + solved * solved
            inverse = lax.rsqrt(spread(pivot, TILE))
            column = {t: rows[k, t] * inverse for t in tiles}
            for t in tiles:
                if t > panel:
                    eliminated[k, t] = column[t]
            for a in range(k + 1, members[-1] + 1):
                factor = spread(column[panel][a - first : a - first + 1, :], TILE)
                for t in tiles:
                    rows[a, t] = rows[a, t] - factor * column[t]


def kernel(
    coords_hbm, obs_hbm, scales_hbm, nugget_hbm, fetch_hbm, slot_hbm,
    white, sums,
    coords, obs, fetch, slots, scales, nugget_s,
    table, looked, asks, asked, answers, far, held, eliminated, part, reduced,
    local_sem, group_send, group_recv, request_sem, reply_sem, reduce_sem,
):
    pts, x = lax.axis_index("pts"), lax.axis_index("grp")
    s, core = pts // 2, pts % 2
    y, z = s // 4, s % 4
    me = 8 * s + 4 * core + x
    mine = 4 * core + x

    def device(offset):
        dy, dz, dcore, dx = offset
        return ((((y + dy) % 4) * 4 + (z + dz) % 4) * 2 + (core + dcore) % 2, (x + dx) % 4)

    across = ((((s + 2 * core + 15) % 16) * 2 + 1 - core), x)

    barrier = pltpu.get_barrier_semaphore()
    peers = [device(o) for o in PLANE] + [device(o) for o in GROUP] + [across]
    for peer in peers:
        pl.semaphore_signal(barrier, 1, device_id=peer, device_id_type=MESH)

    loads = [
        pltpu.make_async_copy(fetch_hbm.at[:, 0, :], fetch, local_sem.at[0]),
        pltpu.make_async_copy(coords_hbm, coords, local_sem.at[1]),
        pltpu.make_async_copy(obs_hbm, obs, local_sem.at[2]),
        pltpu.make_async_copy(slot_hbm, slots, local_sem.at[3]),
        pltpu.make_async_copy(scales_hbm, scales, local_sem.at[4]),
        pltpu.make_async_copy(nugget_hbm, nugget_s, local_sem.at[5]),
    ]
    for load in loads:
        load.start()
    for load in loads:
        load.wait()

    def strip(index):
        return pl.ds(pl.multiple_of(8 * index, 8), 8)

    line = lax.broadcasted_iota(jnp.int32, (LANES, LANES), 0)
    sixteen = jnp.concatenate([fetch[...], jnp.zeros((5, LANES), jnp.int32)], axis=0)
    asks[...] = jnp.where(line // 64 == s % 2, jnp.concatenate([sixteen] * 8, axis=0), 0).T
    for c in range(4):
        for b in range(CHUNKS):
            if c == 3:
                table[c, b, mine] = obs[b : b + 1, :]
            else:
                table[c, b, mine] = coords[c : c + 1, b * LANES : (b + 1) * LANES]
    asked[strip(s), :] = asks[strip(s), :]
    pl.semaphore_wait(barrier, len(peers))

    def remote(src, dst, send, recv, peer):
        return pltpu.make_async_remote_copy(
            src_ref=src, dst_ref=dst, send_sem=send, recv_sem=recv, device_id=peer, device_id_type=MESH
        )

    for slot, peer in [(mine, device(o)) for o in GROUP] + [(8, across)]:
        remote(table.at[:, :, mine], table.at[:, :, slot], group_send, group_recv.at[slot], peer).start()
    for offset in PLANE:
        peer = device(offset)
        remote(
            asks.at[strip(peer[0] // 2), :], asked.at[strip(s), :],
            request_sem.at[0], request_sem.at[1], peer,
        ).start()

    def index_of(chunk):
        itself = POINTS + chunk * LANES + lax.broadcasted_iota(jnp.int32, (2, LANES), 1)
        listed = slots[:, pl.ds(pl.multiple_of(chunk * LANES, LANES), LANES)]
        return jnp.concatenate([listed, itself], axis=0)

    def look_up(index, found, tiles):
        block, lane = index >> 7, index & 127
        for which, slot in tiles:
            for b in range(CHUNKS):
                at = block == CHUNKS * which + b
                for c in range(4):
                    found[c] = jnp.where(at, lanes_of(table[c, b, slot], lane), found[c])
        return found

    def own_rows(chunk, carry):
        found = look_up(index_of(chunk), [jnp.zeros((32, LANES), jnp.float32)] * 4, [(1, mine)])
        for c in range(4):
            looked[chunk, c] = found[c]
        return carry

    lax.fori_loop(0, CHUNKS, own_rows, 0)

    def arrived(slot):
        pltpu.make_async_copy(table.at[:, :, slot], table.at[:, :, slot], group_recv.at[slot]).wait()

    for offset in GROUP:
        _, _, dcore, dx = offset
        arrived(((core + dcore) % 2) * 4 + (x + dx) % 4)
    pltpu.make_async_copy(asked.at[pl.ds(0, 120)], asked.at[pl.ds(0, 120)], request_sem.at[1]).wait()

    owned = [table[r // 4, r % 4, 0:8, 0, :] for r in range(16)]
    part_of = (lax.broadcasted_iota(jnp.int32, TILE, 1) // 16 % 4) * 4
    for p in range(8):
        wanted = asked[16 * p : 16 * p + 8, :] + asked[16 * p + 8 : 16 * p + 16, :]
        key, lane = part_of + (wanted >> 7), wanted & 127
        served = jnp.zeros(TILE, jnp.float32)
        for r in range(16):
            served = jnp.where(key == r, lanes_of(owned[r], lane), served)
        answers[8 * p : 8 * p + 8, :] = served
    far[strip(s), :] = answers[strip(s // 2), :]
    for offset in PLANE:
        peer = device(offset)
        remote(
            answers.at[strip(peer[0] // 4), :], far.at[strip(s), :],
            reply_sem.at[0], reply_sem.at[1], peer,
        ).start()

    factor = [jnp.float32(root_three) / jnp.full((1, LANES), scales[c], jnp.float32) for c in range(3)]
    nugget = nugget_s[0]
    before = core * x + (1 - core) * 8
    after = core * 8 + (1 - core) * (4 + x)

    def near_rows(chunk):
        return look_up(index_of(chunk), [looked[chunk, c] for c in range(4)], [(0, before), (2, after)])

    def finish(found, chunk):
        scaled = [found[c] * factor[c] for c in range(3)]
        for c in range(3):
            held[c] = scaled[c]
        held[3] = found[3]
        return eliminate(scaled, nugget, held, eliminated, white.at[pl.ds(chunk, 1), :])

    def near_chunk(chunk, total):
        return total + finish(near_rows(chunk), chunk)

    arrived(8)
    total = lax.fori_loop(1, CHUNKS, near_chunk, jnp.zeros((1, LANES), jnp.float32))

    found = near_rows(0)
    number = index_of(0) - NEAR
    lane_id = lax.broadcasted_iota(jnp.int32, TILE, 1)
    packed = number[0:8]
    for t in range(1, 4):
        packed = jnp.where(lane_id // EARLY == t, pltpu.roll(number[8 * t : 8 * t + 8], EARLY * t, axis=1), packed)
    owner = (packed * 5958) >> 16
    place = jnp.where(packed >= 0, packed - CAP * owner, -1)
    owner = owner & 127
    is_far = [(number[8 * t : 8 * t + 8] >= 0) & (lane_id < EARLY) for t in range(4)]

    pltpu.make_async_copy(far.at[pl.ds(0, 120)], far.at[pl.ds(0, 120)], reply_sem.at[1]).wait()
    turned = far[...].T
    turned = jnp.where(s % 2 == 1, turned[64:128], turned[0:64])
    for c in range(4):
        fetched = jnp.zeros(TILE, jnp.float32)
        for r in range(CAP):
            fetched = jnp.where(place == r, lanes_of(turned[16 * c + r : 16 * c + r + 1, :], owner), fetched)
        found[c] = jnp.concatenate(
            [
                jnp.where(
                    is_far[t],
                    pltpu.roll(fetched, LANES - EARLY * t, axis=1) if t else fetched,
                    found[c][8 * t : 8 * t + 8],
                )
                for t in range(4)
            ],
            axis=0,
        )
    total = total + finish(found, 0)

    part[0] = total
    reduced[me] = total
    for offset in EVERYONE:
        remote(part.at[0], reduced.at[me], reduce_sem.at[0], reduce_sem.at[1], device(offset)).start()

    pltpu.make_async_copy(table.at[:, :, pl.ds(0, 8)], table.at[:, :, pl.ds(0, 8)], group_send).wait()
    pltpu.make_async_copy(asked.at[pl.ds(0, 120)], asked.at[pl.ds(0, 120)], request_sem.at[0]).wait()
    pltpu.make_async_copy(far.at[pl.ds(0, 120)], far.at[pl.ds(0, 120)], reply_sem.at[0]).wait()
    pltpu.make_async_copy(reduced.at[pl.ds(0, 127)], reduced.at[pl.ds(0, 127)], reduce_sem.at[1]).wait()
    sums[...] = jnp.sum(reduced[...], axis=0)
    pltpu.make_async_copy(reduced.at[pl.ds(0, 127)], reduced.at[pl.ds(0, 127)], reduce_sem.at[0]).wait()


def closing(white, sums, white_hbm, nll_hbm, nll, sem):
    out = pltpu.make_async_copy(white, white_hbm, sem.at[0])
    out.start()
    scale = 1.0 / (2.0 * POINTS * DEVICES)
    nll[...] = jnp.sum(sums[...], axis=1, keepdims=True) * scale + half_log_tau
    nll_out = pltpu.make_async_copy(nll, nll_hbm, sem.at[1])
    nll_out.start()
    out.wait()
    nll_out.wait()


def body(coords, observations, length_scales, nugget, fetch_table, slot_of):
    hbm = pl.BlockSpec(memory_space=pltpu.HBM)
    vmem = pl.BlockSpec(memory_space=pltpu.VMEM)
    white, sums = pl.pallas_call(
        kernel,
        out_shape=(pltpu.VMEM((CHUNKS, LANES), jnp.float32), pltpu.VMEM((1, LANES), jnp.float32)),
        in_specs=[hbm] * 6,
        out_specs=(vmem, vmem),
        scratch_shapes=[
            pltpu.VMEM((3, POINTS), jnp.float32),
            pltpu.VMEM((CHUNKS, LANES), jnp.float32),
            pltpu.VMEM((CAP, LANES), jnp.int32),
            pltpu.VMEM((ORDER - 1, POINTS), jnp.int32),
            pltpu.SMEM((3,), jnp.float32),
            pltpu.SMEM((1,), jnp.float32),
            pltpu.VMEM((4, CHUNKS, 9, 1, LANES), jnp.float32),
            pltpu.VMEM((CHUNKS, 4, 32, LANES), jnp.float32),
            pltpu.VMEM((LANES, LANES), jnp.int32),
            pltpu.VMEM((LANES, LANES), jnp.int32),
            pltpu.VMEM((64, LANES), jnp.float32),
            pltpu.VMEM((LANES, LANES), jnp.float32),
            pltpu.VMEM((4, 32, LANES), jnp.float32),
            pltpu.VMEM((ORDER, 4, 8, LANES), jnp.float32),
            pltpu.VMEM((1, 1, LANES), jnp.float32),
            pltpu.VMEM((DEVICES, 1, LANES), jnp.float32),
            pltpu.SemaphoreType.DMA((6,)),
            pltpu.SemaphoreType.DMA,
            pltpu.SemaphoreType.DMA((9,)),
            pltpu.SemaphoreType.DMA((2,)),
            pltpu.SemaphoreType.DMA((2,)),
            pltpu.SemaphoreType.DMA((2,)),
        ],
        compiler_params=pltpu.CompilerParams(collective_id=0, has_side_effects=True),
        name="vecchia",
    )(
        coords,
        observations.reshape(CHUNKS, LANES),
        length_scales,
        nugget,
        jnp.transpose(fetch_table, (2, 0, 1)),
        slot_of,
    )
    white, nll = pl.pallas_call(
        closing,
        out_shape=(
            jax.ShapeDtypeStruct((CHUNKS, LANES), jnp.float32),
            jax.ShapeDtypeStruct((1, 1), jnp.float32),
        ),
        in_specs=[vmem, vmem],
        out_specs=(hbm, hbm),
        scratch_shapes=[pltpu.VMEM((1, 1), jnp.float32), pltpu.SemaphoreType.DMA((2,))],
        name="closing",
    )(pltpu.with_memory_space_constraint(white, pltpu.VMEM), pltpu.with_memory_space_constraint(sums, pltpu.VMEM))
    return white.reshape(POINTS), nll.reshape(())


def solution(mesh):
    return jax.shard_map(
        body,
        mesh=mesh,
        in_specs=(P(None, ALL), P(ALL), P(), P(), P(ALL, None, None), P(None, ALL)),
        out_specs=(P(ALL), P()),
        check_vma=False,
    )
```

time: 31 us -> 26.8 us (0.86)
  local copies, waits for them, and re-layouts: 2.54 us -> 0 us
  between operations: 2.46 us -> 1.28 us
  Pallas kernels: 25.8 us -> 25.3 us
    unnamed x6 -> x0, local copies, waits for them, and re-layouts: 2.54 us -> none
    pallas_call x1 -> x2, Pallas kernels: 25.8 us -> 25.3 us  [the longest x1 24.7 us: body(): pl.pallas_call(kernel, out_shape=(pltpu.VMEM((CHUNKS, LANES), jnp.float32...]
where the time goes in v2:
time: 26.8 us; the launch traced here: 26.6 us
  Pallas kernels  25.3 us (94%)
  between operations  1.28 us (5%)
    pallas_call x1, Pallas kernels, body(): pl.pallas_call(kernel, out_shape=(pltpu.VMEM((CHUNKS, LANES), jnp.float32...  24.7 us
    pallas_call x1, Pallas kernels, body(): pl.pallas_call(closing, out_shape=(jax.ShapeDtypeStruct((CHUNKS, LANES),...  0.61 us

profile of v2, /device:TPU:1, one launch (start us, length us, event | category | flops | bytes accessed | tf_op | source)
XLA Modules:
  0.0 26.6 jit_solution(3549913003064088968)
XLA Ops:
  1.3 24.7 %vecchia.1 = (f32[4,128]{1,0:T(4,128)S(1)}, f32[1,128]{1,0:T(1,128)S(1)}) custom-call(f32[3,512]{1,0:T(4,128)} %coords_hbm.1, f32[4,128]{1,0:T(4,128)} %bitcast.5, f32[3]{0:T(128)} %scales_hbm.1, f32[1]{0:T(128)S(6)} %copy.8.nugget_hbm, s32[11,1,128]{2,1,0:T(1,128)} %bitcast.4, s32[30,512]{1,0:T(8,128)} %slot_hbm.1), custom_call_target="tpu_custom_call" | custom-call | tf_op jit(solution)/shard_map/vecchia/pallas_call | solution.py:291
  26.0 0.6 %closing.1 = (f32[4,128]{1,0:T(4,128)}, f32[1,1]{1,0:T(1,128)}) custom-call(f32[4,128]{1,0:T(4,128)S(1)} %get-tuple-element.6.white, f32[1,128]{1,0:T(1,128)S(1)} %get-tuple-element.7.sums), custom_call_target="tpu_custom_call" | custom-call | tf_op jit(solution)/shard_map/closing/pallas_call | solution.py:330
